TPU v7x, 32 devices: a whole 2x2x4 slice. The times are simulated.
32 devices in a mesh: fsdp: 8 (over z, y), tp: 4 (over x, core).
Axes of the slice: x: 2, y: 2, z: 4, core: 2. Of those that a mesh axis runs over, the one named last changes fastest.
Arguments:
- hidden_in: bfloat16 [1024, 8192], P('fsdp'), may hold values from -6 to 6
- key_grad: bfloat16 [1024, 1024], P('fsdp', 'tp'), may hold values from -2.5 to 2.5
- positions: int32 [1024], P('fsdp'), may hold values from 0 to 1023, as said below
- key_quant: bfloat16 [8704, 1024], P('fsdp', 'tp'), may hold values from -4 to 4
- key_scales: float32 [8704, 8], P('fsdp', 'tp'), may hold values from 0.01 to 0.1
- block_counts: int32 [8], replicated, may hold values from 960 to 1088, as said below
Outputs:
- weight_grad: bfloat16 [8704, 1024], P('fsdp', 'tp')
- input_grad: bfloat16 [1024, 8192], P('fsdp', 'tp')
Inputs may be any that keep to these rules, and one draw needn't show every extreme that they name: Index f of fsdp owns the consecutive projection rows from block_counts[0] + ... + block_counts[f-1] on, in its first block_counts[f] slots; the counts sum to 8192, and some index owns exactly 1088 rows. positions count the tokens from the start of their packed document; the first token's document may have begun before the first token, and a document may go on into the next index's tokens.
All inputs are finite; a program needn't handle non-finite values.
Results may differ from a plain program's by a relative error of at most 0.013.
Values may be sent and summed in bfloat16 or wider, within the bound.
A program may use at most 64 MiB of HBM per device.

v0:
```python
import math
import jax
import jax.numpy as jnp
from jax import lax
from jax.sharding import PartitionSpec as P

HD = 128
rope_base = 500000.0


def rotary_backward(key_grad, positions):
    tokens_here = key_grad.shape[0]
    half_dim = HD // 2
    cotangent = key_grad.astype(jnp.float32).reshape(tokens_here, -1, HD)
    freq_idx = jnp.arange(half_dim, dtype=jnp.float32)
    inverse = jnp.exp(-(2.0 * freq_idx / HD) * math.log(rope_base))
    angles = positions.astype(jnp.float32)[:, None] * inverse[None, :]
    cosine = jnp.cos(angles)[:, None, :]
    sine_part = jnp.sin(angles)[:, None, :]
    lower_half = cotangent[..., :half_dim]
    upper_half = cotangent[..., half_dim:]
    back_lower = lower_half * cosine + upper_half * sine_part
    back_upper = upper_half * cosine - lower_half * sine_part
    joined = jnp.concatenate([back_lower, back_upper], axis=-1)
    return joined.reshape(tokens_here, -1).astype(jnp.bfloat16)


def slot_tables(block_counts, slot_count, row_total):
    offsets = jnp.cumsum(block_counts) - block_counts
    owners_n = block_counts.shape[0]
    slot_ids = jnp.arange(owners_n * slot_count, dtype=jnp.int32)
    within = slot_ids % slot_count
    live_counts = jnp.broadcast_to(block_counts[:, None], (owners_n, slot_count)).reshape(-1)
    base_rows = jnp.broadcast_to(offsets[:, None], (owners_n, slot_count)).reshape(-1)
    is_live = within < live_counts
    row_of_slot = jnp.where(is_live, base_rows + within, 0)
    row_ids = jnp.arange(row_total, dtype=jnp.int32)
    at_or_after = row_ids[:, None] >= offsets[None, :]
    owner_of_row = jnp.sum(at_or_after.astype(jnp.int32), axis=1) - 1
    row_begin = jnp.max(jnp.where(at_or_after, offsets[None, :], 0), axis=1)
    slot_of_row = owner_of_row * slot_count + row_ids - row_begin
    return (row_of_slot, is_live, slot_of_row)


def per_device(hidden_in, key_grad, positions, key_quant, key_scales, block_counts):
    slot_count = key_quant.shape[0]
    local_heads = key_scales.shape[1]
    row_total = hidden_in.shape[1]
    row_of_slot, is_live, slot_of_row = slot_tables(block_counts, slot_count, row_total)
    scaled = (
        key_quant.astype(jnp.float32).reshape(slot_count, local_heads, HD) * key_scales[:, :, None]
    )
    local_weights = scaled.astype(jnp.bfloat16).reshape(slot_count, local_heads * HD)
    rotated = rotary_backward(key_grad, positions)
    picked = jnp.where(
        is_live[None, :], jnp.take(hidden_in, row_of_slot, axis=1), jnp.zeros((), jnp.bfloat16)
    )
    weight_grad = lax.psum_scatter(
        lax.dot_general(
            picked, rotated, (((0,), (0,)), ((), ())), preferred_element_type=jnp.float32
        ),
        "fsdp",
        scatter_dimension=0,
        tiled=True,
    ).astype(jnp.bfloat16)
    group_total = lax.axis_size("tp")
    whole_slots = lax.all_gather(local_weights, "fsdp", axis=0, tiled=True)
    ordered = jnp.take(whole_slots, slot_of_row, axis=0)
    own_rows = lax.all_to_all(ordered, "tp", split_axis=0, concat_axis=1, tiled=True)
    all_heads = lax.all_gather(rotated, "tp", axis=1, tiled=True)
    tokens_here = all_heads.shape[0]
    feature_here = own_rows.shape[0]
    heads_grouped = all_heads.reshape(tokens_here, group_total, -1)
    rows_grouped = own_rows.reshape(feature_here, group_total, -1)
    group_part = jnp.einsum(
        "tgk,dgk->gtd", heads_grouped, rows_grouped, preferred_element_type=jnp.float32
    ).astype(jnp.bfloat16)
    input_grad = jnp.sum(group_part.astype(jnp.float32), axis=0).astype(jnp.bfloat16)
    return (weight_grad, input_grad)


def solution(mesh):
    in_specs = (P("fsdp", None), P("fsdp", "tp"), P("fsdp"), P("fsdp", "tp"), P("fsdp", "tp"), P())
    out_specs = (P("fsdp", "tp"), P("fsdp", "tp"))
    return jax.shard_map(
        per_device, mesh=mesh, in_specs=in_specs, out_specs=out_specs, check_vma=False
    )
```

profile of v0, /device:TPU:0, one launch (start us, length us, event | category | flops | bytes accessed | tf_op | source)
XLA Modules:
  0.0 256.9 jit_solution(10514191697717490936)
XLA Ops:
  7.2 0.0 all-gather.2.cloned.1.call-start
  7.2 1.0 copy.18
  8.2 0.0 copy-start.2
  8.2 0.0 copy-start.1
  8.2 2.5 mul.108
  10.8 0.9 fusion.13
  11.7 0.0 all-gather.2.cloned.1.call-update
  11.7 0.0 reduce-scatter.2.cloned.1.call-start
  11.8 0.2 reduce-window.9
  12.0 0.1 broadcast_in_dim.67
  12.1 0.1 reshape.253
  12.2 0.1 reshape.251
  12.2 0.1 broadcast_in_dim.65
  12.3 0.1 reshape.252
  12.4 0.1 reshape.248
  12.5 0.1 copy.21
  12.6 3.2 %copy.15 = bf16[128,8192]{0,1:T(8,128)(2,1)S(1)} copy(bf16[128,8192]{1,0:T(8,128)(2,1)} %param.6) | data formatting | bytes 4194304 | tf_op args[0]
  15.9 0.2 fusion.20
  16.1 18.3 %gather_fusion = bf16[8704,128]{1,0:T(8,128)(2,1)} fusion(bf16[128,8192]{0,1:T(8,128)(2,1)S(1)} %copy.15, s32[9216]{0:T(1024)S(1)} %pad_clamp_fusion), kind=kCustom, calls=%fused_computation | custom fusion | bytes 4491264 | tf_op jit(solution)/shard_map/jit(_take)/gather | solution.py:56
  34.4 0.2 multiply_cosine_fusion
  34.7 8.8 %fusion.5 = f32[8704,256]{1,0:T(8,128)} fusion(bf16[128,256]{0,1:T(8,128)(2,1)S(1)} %bitcast.27, bf16[8704,128]{1,0:T(8,128)(2,1)} %gather_fusion, pred[8704]{0:T(1024)(128)(4,1)S(1)} %get-tuple-element.5, pred[8704]{0:T(1024)(128)(4,1)S(1)} %get-tuple-element.4), kind=kOutput, calls=%fused_computation.6 | convolution fusion | flops 572653568 | bytes 11224064 | tf_op jit(solution)/shard_map/dot_general | solution.py:59
  43.5 0.0 reduce-scatter.2.cloned.1.call-update
  43.5 0.3 convert_reduce_fusion
  43.9 0.1 compare_select_fusion.1
  44.0 46.7 %all-gather.2.cloned.1.call-done = bf16[8704,256]{1,0:T(8,128)(2,1)} async-done(((bf16[1088,256]{1,0:T(8,128)(2,1)}), bf16[8704,256]{1,0:T(8,128)(2,1)}) %all-gather.2.cloned.1.call-update) | async-done | bytes 4456464 | tf_op jit(solution)/shard_map/all_gather | solution.py:67
  90.7 33.7 %gather_fusion.1 = bf16[8192,256]{1,0:T(8,128)(2,1)} fusion(bf16[8704,256]{1,0:T(8,128)(2,1)} %all-gather.2.cloned.1.call-done, s32[8192]{0:T(1024)S(1)} %broadcast_clamp_fusion), kind=kCustom, calls=%fused_computation.1 | custom fusion | bytes 8421376 | tf_op jit(solution)/shard_map/jit(_take)/gather | solution.py:68
  124.4 5.3 %broadcast_select_fusion = bf16[4,2048,256]{2,1,0:T(8,128)(2,1)} fusion(bf16[4,2048,256]{2,1,0:T(8,128)(2,1)} %bitcast.24, pred[4,2048]{1,0:T(4,128)(4,1)S(1)} %compare_and_fusion.1), kind=kLoop, calls=%fused_computation.4 | loop fusion | flops 2097152 | bytes 8396800 | tf_op jit(solution)/shard_map/jit(_take)/select_n | solution.py:68
  129.7 4.9 %all-to-all-start = ((bf16[4,2048,256]{2,1,0:T(8,128)(2,1)}), bf16[4,2048,256]{2,1,0:T(8,128)(2,1)}, u32[]{:S(2)}, u32[]{:S(2)}) async-start(bf16[4,2048,256]{2,1,0:T(8,128)(2,1)} %broadcast_select_fusion), calls=%async_computation.1 | async-start | bytes 8388608 | tf_op jit(solution)/shard_map/all_to_all | solution.py:69
  134.6 50.3 %all_gather.6 = bf16[128,1024]{0,1:T(8,128)(2,1)S(1)} all-gather(bf16[128,256]{0,1:T(8,128)(2,1)S(1)} %bitcast.28), channel_id=1, replica_groups=mesh['fsdp'=8,'tp'=4] {'tp'}, dimensions={1}, use_global_device_ids=true | all-gather | bytes 327680 | tf_op jit(solution)/shard_map/all_gather | solution.py:70
  184.9 4.8 %fusion.10 = bf16[128,2048]{1,0:T(8,128)(2,1)} fusion(bf16[128,4,256]{0,2,1:T(8,128)(2,1)S(1)} %bitcast.26, bf16[4,2048,256]{2,1,0:T(8,128)(2,1)} %all-to-all-done), kind=kOutput, calls=%fused_computation.11 | convolution fusion | flops 538705920 | bytes 4980736 | tf_op jit(solution)/shard_map/tgk,dgk->gtd/dot_general | solution.py:75
  189.7 58.2 %reduce-scatter.2.cloned.1.call-done = f32[1088,256]{1,0:T(8,128)} async-done(((f32[8704,256]{1,0:T(8,128)}), f32[1088,256]{1,0:T(8,128)}) %reduce-scatter.2.cloned.1.call-update) | async-done | bytes 1114128 | tf_op jit(solution)/shard_map/reduce_scatter | solution.py:58
  248.0 2.1 convert_element_type.28
  (19 shorter events, 0.2 us)
Async XLA Ops:
  7.2 3.6 %copy-start = (bf16[1088,256]{1,0:T(8,128)(2,1)S(1)}, bf16[1088,256]{1,0:T(8,128)(2,1)}, u32[]{:S(2)}) copy-start(bf16[1088,256]{1,0:T(8,128)(2,1)} %param.9) | copy-start | bytes 1671172
  7.2 83.5 %all-gather.2.cloned.1.call-start = ((), (), s32[]{:S(2)}) async-start(), calls=%async_computation.3 | async-start | bytes 5013504 | tf_op jit(solution)/shard_map/all_gather | solution.py:67
  8.2 3.6 %copy-start.2 = (s32[8]{0:T(128)S(1)}, s32[8]{0:T(128)}, u32[]{:S(2)}) copy-start(s32[8]{0:T(128)} %param.11) | copy-start | bytes 100
  8.2 4.3 %copy-start.1 = (bf16[128,256]{1,0:T(8,128)(2,1)S(1)}, bf16[128,256]{1,0:T(8,128)(2,1)}, u32[]{:S(2)}) copy-start(bf16[128,256]{1,0:T(8,128)(2,1)} %param.7) | copy-start | bytes 196612
  8.2 4.4 %copy-start.3 = (s32[128]{0:T(128)S(1)}, s32[128]{0:T(128)}, u32[]{:S(2)}) copy-start(s32[128]{0:T(128)} %param.8) | copy-start | bytes 1540
  11.7 236.3 %reduce-scatter.2.cloned.1.call-start = ((), (), s32[]{:S(2)}) async-start(), calls=%async_computation.2 | async-start | bytes 10027008 | tf_op jit(solution)/shard_map/reduce_scatter | solution.py:58
  129.7 55.2 %all-to-all-start = ((bf16[4,2048,256]{2,1,0:T(8,128)(2,1)}), bf16[4,2048,256]{2,1,0:T(8,128)(2,1)}, u32[]{:S(2)}, u32[]{:S(2)}) async-start(bf16[4,2048,256]{2,1,0:T(8,128)(2,1)} %broadcast_select_fusion), calls=%async_computation.1 | async-start | bytes 8388608 | tf_op jit(solution)/shard_map/all_to_all | solution.py:69
Sparse Core Ops, SparseCore 0:
  11.9 78.7 all-gather.1
  94.3 153.6 reduce-scatter.1
where the time goes:
time: 258 us; the launch traced here: 257 us
  waiting for transfers between devices  105 us (41%)
  local copies, waits for them, and re-layouts  59.4 us (23%)
  blocking collectives  50.3 us (19%)
  between operations  14.2 us (6%)
  matrix products  13.6 us (5%)
  other arithmetic  9.44 us (4%)
  starting transfers between devices  4.98 us (2%)
    reduce_scatter x1, waiting for transfers between devices, per_device(): lax.psum_scatter(lax.dot_general(picked, rotated, (((0,), (0,)), ((), ())...  58.2 us
    all_gather x1, blocking collectives, per_device(): all_heads = lax.all_gather(rotated, 'tp', axis=1, tiled=True)  50.3 us
    all_gather x1, waiting for transfers between devices, per_device(): whole_slots = lax.all_gather(local_weights, 'fsdp', axis=0, tiled=True)  46.7 us
    gather x1, local copies, waits for them, and re-layouts, per_device(): ordered = jnp.take(whole_slots, slot_of_row, axis=0)  33.7 us
    gather x1, local copies, waits for them, and re-layouts, per_device(): jnp.take(hidden_in, row_of_slot, axis=1)  18.3 us
    dot_general x1, matrix products, per_device(): lax.dot_general(picked, rotated, (((0,), (0,)), ((), ())), preferred_elem...  8.82 us
    select_n x2, other arithmetic, per_device(): ordered = jnp.take(whole_slots, slot_of_row, axis=0)  5.34 us
  transfers between devices with their start and end apart: 3, of which 2 were waited for; matrix products, arithmetic and copies ran while one was open for 30% of the time, Pallas kernels for 0%

commit v1 on v0

--- a/solution.py
+++ b/solution.py
@@ -64,7 +64,27 @@
         tiled=True,
     ).astype(jnp.bfloat16)
     group_total = lax.axis_size("tp")
-    whole_slots = lax.all_gather(local_weights, "fsdp", axis=0, tiled=True)
+    length, index, width = (lax.axis_size("fsdp"), lax.axis_index("fsdp"), local_weights.shape[0])
+    right = [(i, (i + 1) % length) for i in range(length)]
+    left = [(i, (i - 1) % length) for i in range(length)]
+    filled = jnp.zeros(
+        (*local_weights.shape[:0], length * width, *local_weights.shape[0 + 1 :]),
+        local_weights.dtype,
+    )
+    filled = lax.dynamic_update_slice_in_dim(filled, local_weights, index * width, axis=0)
+    from_left = from_right = local_weights
+    halfway = length // 2
+    for step in range(1, halfway + 1):
+        from_left = lax.ppermute(from_left, "fsdp", right)
+        filled = lax.dynamic_update_slice_in_dim(
+            filled, from_left, (index - step) % length * width, axis=0
+        )
+        if step < length - halfway:
+            from_right = lax.ppermute(from_right, "fsdp", left)
+            filled = lax.dynamic_update_slice_in_dim(
+                filled, from_right, (index + step) % length * width, axis=0
+            )
+    whole_slots = filled
     ordered = jnp.take(whole_slots, slot_of_row, axis=0)
     own_rows = lax.all_to_all(ordered, "tp", split_axis=0, concat_axis=1, tiled=True)
     all_heads = lax.all_gather(rotated, "tp", axis=1, tiled=True)

time: 258 us -> 293 us (1.14); the launches traced: 257 us -> 289 us
  starting transfers between devices: 4.98 us -> 22 us
  local copies, waits for them, and re-layouts: 59.4 us -> 69 us
  waiting for transfers between devices: 105 us -> 108 us
    ppermute x0 -> x7, waiting for transfers between devices: none -> 108 us  [the longest x4 105 us: per_device(): from_left = lax.ppermute(from_left, 'fsdp', right)]
    reduce_scatter x1, waiting for transfers between devices: 58.2 us -> 0.01 us  [per_device(): lax.psum_scatter(lax.dot_general(picked, rotated, (((0,), (0,)), ((), ())...]
    all_gather x1 -> x0, waiting for transfers between devices: 46.7 us -> none  [per_device(): whole_slots = lax.all_gather(local_weights, 'fsdp', axis=0, tiled=True)]
    ppermute x0 -> x7, starting transfers between devices: none -> 17.1 us  [the longest x3 11.7 us: per_device(): from_right = lax.ppermute(from_right, 'fsdp', left)]
    dynamic_update_slice x0 -> x7, local copies, waits for them, and re-layouts: none -> 5.93 us  [the longest x4 3.42 us: per_device(): lax.dynamic_update_slice_in_dim(filled, from_left, (index - step) % lengt...]
  transfers between devices with their start and end apart: 3 -> 9, of which waited for: 2 -> 6; matrix products, arithmetic and copies ran while one was open for 30% -> 19% of each run, Pallas kernels for 0% -> 0%
where the time goes in v1:
time: 293 us; the launch traced here: 289 us
  waiting for transfers between devices  108 us (37%)
  local copies, waits for them, and re-layouts  69 us (24%)
  blocking collectives  50.3 us (17%)
  starting transfers between devices  22 us (8%)
  between operations  14.2 us (5%)
  matrix products  13.4 us (5%)
  other arithmetic  11.7 us (4%)
    ppermute x4, waiting for transfers between devices, per_device(): from_left = lax.ppermute(from_left, 'fsdp', right)  105 us
    all_gather x1, blocking collectives, per_device(): all_heads = lax.all_gather(rotated, 'tp', axis=1, tiled=True)  50.3 us
    gather x1, local copies, waits for them, and re-layouts, per_device(): ordered = jnp.take(whole_slots, slot_of_row, axis=0)  33.7 us
    gather x1, local copies, waits for them, and re-layouts, per_device(): jnp.take(hidden_in, row_of_slot, axis=1)  18.3 us
    ppermute x3, starting transfers between devices, per_device(): from_right = lax.ppermute(from_right, 'fsdp', left)  11.7 us
    dot_general x1, matrix products, per_device(): lax.dot_general(picked, rotated, (((0,), (0,)), ((), ())), preferred_elem...  8.8 us
  transfers between devices with their start and end apart: 9, of which 6 were waited for; matrix products, arithmetic and copies ran while one was open for 19% of the time, Pallas kernels for 0%

profile of v1, /device:TPU:0, one launch (start us, length us, event | category | flops | bytes accessed | tf_op | source)
XLA Modules:
  0.0 288.7 jit_solution(4815059940981942307)
XLA Ops:
  7.2 0.8 reduce-window.9
  9.9 0.9 copy.21
  11.5 3.2 %copy.15 = bf16[128,8192]{0,1:T(8,128)(2,1)S(1)} copy(bf16[128,8192]{1,0:T(8,128)(2,1)} %param.6) | data formatting | bytes 4194304 | tf_op args[0]
  15.2 18.3 %gather_fusion = bf16[8704,128]{1,0:T(8,128)(2,1)} fusion(bf16[128,8192]{0,1:T(8,128)(2,1)S(1)} %copy.15, s32[9216]{0:T(1024)S(1)} %pad_clamp_fusion), kind=kCustom, calls=%fused_computation | custom fusion | bytes 4491264 | tf_op jit(solution)/shard_map/jit(_take)/gather | solution.py:56
  33.5 8.8 %fusion.5 = f32[8704,256]{1,0:T(8,128)} fusion(bf16[128,256]{0,1:T(8,128)(2,1)S(1)} %bitcast.28, bf16[8704,128]{1,0:T(8,128)(2,1)} %gather_fusion, pred[8704]{0:T(1024)(128)(4,1)S(1)} %get-tuple-element.7, pred[8704]{0:T(1024)(128)(4,1)S(1)} %get-tuple-element.6), kind=kOutput, calls=%fused_computation.6 | convolution fusion | flops 572653568 | bytes 11224064 | tf_op jit(solution)/shard_map/dot_general | solution.py:59
  43.3 2.5 mul.132
  45.8 2.3 broadcast_in_dim.76
  48.1 1.1 constant_dynamic-update-slice_fusion.7
  49.2 2.9 %collective-permute-start = (bf16[1088,256]{1,0:T(8,128)(2,1)S(1)}, bf16[1088,256]{1,0:T(8,128)(2,1)S(1)}, u32[]{:S(2)}, u32[]{:S(2)}) collective-permute-start(bf16[1088,256]{1,0:T(8,128)(2,1)S(1)} %get-tuple-element.5), channel_id=1, source_target_pairs={{0,4},{4,8},{8,12},{12,16},{16,20},{20,24},{24,28},{28,0},{1,5},{5... | collective-permute-start | bytes 1671176 | tf_op jit(solution)/shard_map/ppermute | solution.py:78
  52.1 3.1 %collective-permute-start.1 = (bf16[1088,256]{1,0:T(8,128)(2,1)S(1)}, bf16[1088,256]{1,0:T(8,128)(2,1)S(1)}, u32[]{:S(2)}, u32[]{:S(2)}) collective-permute-start(bf16[1088,256]{1,0:T(8,128)(2,1)S(1)} %get-tuple-element.5), channel_id=1, source_target_pairs={{0,28},{4,0},{8,4},{12,8},{16,12},{20,16},{24,20},{28,24},{1,29},{... | collective-permute-start | bytes 1671176 | tf_op jit(solution)/shard_map/ppermute | solution.py:83
  55.6 32.3 %collective-permute-done = bf16[1088,256]{1,0:T(8,128)(2,1)S(1)} collective-permute-done((bf16[1088,256]{1,0:T(8,128)(2,1)S(1)}, bf16[1088,256]{1,0:T(8,128)(2,1)S(1)}, u32[]{:S(2)}, u32[]{:S(2)}) %collective-permute-start) | collective-permute-done | bytes 557088 | tf_op jit(solution)/shard_map/ppermute | solution.py:78
  87.8 2.5 collective-permute-start.2
  90.4 3.1 %collective-permute-start.3 = (bf16[1088,256]{1,0:T(8,128)(2,1)S(1)}, bf16[1088,256]{1,0:T(8,128)(2,1)S(1)}, u32[]{:S(2)}, u32[]{:S(2)}) collective-permute-start(bf16[1088,256]{1,0:T(8,128)(2,1)S(1)} %collective-permute-done.1), channel_id=1, source_target_pairs={{0,28},{4,0},{8,4},{12,8},{16,12},{20,16},{24,20},{28,24},{1,29},{... | collective-permute-start | bytes 1671176 | tf_op jit(solution)/shard_map/ppermute | solution.py:83
  93.5 24.1 %collective-permute-done.2 = bf16[1088,256]{1,0:T(8,128)(2,1)S(1)} collective-permute-done((bf16[1088,256]{1,0:T(8,128)(2,1)S(1)}, bf16[1088,256]{1,0:T(8,128)(2,1)S(1)}, u32[]{:S(2)}, u32[]{:S(2)}) %collective-permute-start.2) | collective-permute-done | bytes 557088 | tf_op jit(solution)/shard_map/ppermute | solution.py:78
  117.6 0.9 constant_dynamic-update-slice_fusion.6
  118.5 0.8 constant_dynamic-update-slice_fusion.5
  119.3 1.3 collective-permute-done.3
  120.6 5.4 %collective-permute-start.5 = (bf16[1088,256]{1,0:T(8,128)(2,1)S(1)}, bf16[1088,256]{1,0:T(8,128)(2,1)S(1)}, u32[]{:S(2)}, u32[]{:S(2)}) collective-permute-start(bf16[1088,256]{1,0:T(8,128)(2,1)S(1)} %collective-permute-done.3), channel_id=1, source_target_pairs={{0,28},{4,0},{8,4},{12,8},{16,12},{20,16},{24,20},{28,24},{1,29},{... | collective-permute-start | bytes 1671176 | tf_op jit(solution)/shard_map/ppermute | solution.py:83
  126.1 0.8 constant_dynamic-update-slice_fusion.4
  126.9 21.0 %collective-permute-done.4 = bf16[1088,256]{1,0:T(8,128)(2,1)S(1)} collective-permute-done((bf16[1088,256]{1,0:T(8,128)(2,1)S(1)}, bf16[1088,256]{1,0:T(8,128)(2,1)S(1)}, u32[]{:S(2)}, u32[]{:S(2)}) %collective-permute-start.4) | collective-permute-done | bytes 557088 | tf_op jit(solution)/shard_map/ppermute | solution.py:78
  147.9 0.8 constant_dynamic-update-slice_fusion.3
  148.8 0.9 constant_dynamic-update-slice_fusion.2
  149.6 2.1 collective-permute-done.5
  151.7 0.9 constant_dynamic-update-slice_fusion.1
  152.6 27.3 %collective-permute-done.6 = bf16[1088,256]{1,0:T(8,128)(2,1)S(1)} collective-permute-done((bf16[1088,256]{1,0:T(8,128)(2,1)S(1)}, bf16[1088,256]{1,0:T(8,128)(2,1)S(1)}, u32[]{:S(2)}, u32[]{:S(2)}) %collective-permute-start.6) | collective-permute-done | bytes 557088 | tf_op jit(solution)/shard_map/ppermute | solution.py:78
  179.9 0.8 constant_dynamic-update-slice_fusion
  180.7 33.7 %gather_fusion.1 = bf16[8192,256]{1,0:T(8,128)(2,1)} fusion(bf16[8704,256]{1,0:T(8,128)(2,1)} %constant_dynamic-update-slice_fusion, s32[8192]{0:T(1024)S(1)} %broadcast_clamp_fusion), kind=kCustom, calls=%fused_computation.1 | custom fusion | bytes 8421376 | tf_op jit(solution)/shard_map/jit(_take)/gather | solution.py:88
  214.4 5.5 %broadcast_select_fusion = bf16[4,2048,256]{2,1,0:T(8,128)(2,1)} fusion(bf16[4,2048,256]{2,1,0:T(8,128)(2,1)} %bitcast.25, pred[4,2048]{1,0:T(4,128)(4,1)S(1)} %compare_and_fusion.1), kind=kLoop, calls=%fused_computation.4 | loop fusion | flops 2097152 | bytes 8396800 | tf_op jit(solution)/shard_map/jit(_take)/select_n | solution.py:88
  219.9 4.9 %all-to-all-start = ((bf16[4,2048,256]{2,1,0:T(8,128)(2,1)}), bf16[4,2048,256]{2,1,0:T(8,128)(2,1)}, u32[]{:S(2)}, u32[]{:S(2)}) async-start(bf16[4,2048,256]{2,1,0:T(8,128)(2,1)} %broadcast_select_fusion), calls=%async_computation.1 | async-start | bytes 8388608 | tf_op jit(solution)/shard_map/all_to_all | solution.py:89
  224.8 50.3 %all_gather.3 = bf16[128,1024]{0,1:T(8,128)(2,1)S(1)} all-gather(bf16[128,256]{0,1:T(8,128)(2,1)S(1)} %bitcast.29), channel_id=1, replica_groups=mesh['fsdp'=8,'tp'=4] {'tp'}, dimensions={1}, use_global_device_ids=true | all-gather | bytes 327680 | tf_op jit(solution)/shard_map/all_gather | solution.py:90
  275.2 4.6 %fusion.10 = bf16[128,2048]{1,0:T(8,128)(2,1)} fusion(bf16[128,4,256]{0,2,1:T(8,128)(2,1)S(1)} %bitcast.27, bf16[4,2048,256]{2,1,0:T(8,128)(2,1)} %all-to-all-done), kind=kOutput, calls=%fused_computation.11 | convolution fusion | flops 538705920 | bytes 4980736 | tf_op jit(solution)/shard_map/tgk,dgk->gtd/dot_general | solution.py:95
  279.8 2.1 convert_element_type.28
  (34 shorter events, 4.4 us)
Async XLA Ops:
  7.2 272.6 %reduce-scatter.2.cloned.1.call-start = ((), (), s32[]{:S(2)}) async-start(), calls=%async_computation.2 | async-start | bytes 10027008 | tf_op jit(solution)/shard_map/reduce_scatter | solution.py:58
  42.3 0.7 copy-start.1
  42.4 5.7 %copy-start = (bf16[1088,256]{1,0:T(8,128)(2,1)S(1)}, bf16[1088,256]{1,0:T(8,128)(2,1)}, u32[]{:S(2)}) copy-start(bf16[1088,256]{1,0:T(8,128)(2,1)} %param.9) | copy-start | bytes 1671172
  49.2 38.7 %collective-permute-start = (bf16[1088,256]{1,0:T(8,128)(2,1)S(1)}, bf16[1088,256]{1,0:T(8,128)(2,1)S(1)}, u32[]{:S(2)}, u32[]{:S(2)}) collective-permute-start(bf16[1088,256]{1,0:T(8,128)(2,1)S(1)} %get-tuple-element.5), channel_id=1, source_target_pairs={{0,4},{4,8},{8,12},{12,16},{16,20},{20,24},{24,28},{28,0},{1,5},{5... | collective-permute-start | bytes 1671176 | tf_op jit(solution)/shard_map/ppermute | solution.py:78
  52.1 38.3 %collective-permute-start.1 = (bf16[1088,256]{1,0:T(8,128)(2,1)S(1)}, bf16[1088,256]{1,0:T(8,128)(2,1)S(1)}, u32[]{:S(2)}, u32[]{:S(2)}) collective-permute-start(bf16[1088,256]{1,0:T(8,128)(2,1)S(1)} %get-tuple-element.5), channel_id=1, source_target_pairs={{0,28},{4,0},{8,4},{12,8},{16,12},{20,16},{24,20},{28,24},{1,29},{... | collective-permute-start | bytes 1671176 | tf_op jit(solution)/shard_map/ppermute | solution.py:83
  87.8 29.8 %collective-permute-start.2 = (bf16[1088,256]{1,0:T(8,128)(2,1)S(1)}, bf16[1088,256]{1,0:T(8,128)(2,1)S(1)}, u32[]{:S(2)}, u32[]{:S(2)}) collective-permute-start(bf16[1088,256]{1,0:T(8,128)(2,1)S(1)} %collective-permute-done), channel_id=1, source_target_pairs={{0,4},{4,8},{8,12},{12,16},{16,20},{20,24},{24,28},{28,0},{1,5},{5... | collective-permute-start | bytes 1671176 | tf_op jit(solution)/shard_map/ppermute | solution.py:78
  90.4 30.3 %collective-permute-start.3 = (bf16[1088,256]{1,0:T(8,128)(2,1)S(1)}, bf16[1088,256]{1,0:T(8,128)(2,1)S(1)}, u32[]{:S(2)}, u32[]{:S(2)}) collective-permute-start(bf16[1088,256]{1,0:T(8,128)(2,1)S(1)} %collective-permute-done.1), channel_id=1, source_target_pairs={{0,28},{4,0},{8,4},{12,8},{16,12},{20,16},{24,20},{28,24},{1,29},{... | collective-permute-start | bytes 1671176 | tf_op jit(solution)/shard_map/ppermute | solution.py:83
  117.6 30.3 %collective-permute-start.4 = (bf16[1088,256]{1,0:T(8,128)(2,1)S(1)}, bf16[1088,256]{1,0:T(8,128)(2,1)S(1)}, u32[]{:S(2)}, u32[]{:S(2)}) collective-permute-start(bf16[1088,256]{1,0:T(8,128)(2,1)S(1)} %collective-permute-done.2), channel_id=1, source_target_pairs={{0,4},{4,8},{8,12},{12,16},{16,20},{20,24},{24,28},{28,0},{1,5},{5... | collective-permute-start | bytes 1671176 | tf_op jit(solution)/shard_map/ppermute | solution.py:78
  120.6 31.1 %collective-permute-start.5 = (bf16[1088,256]{1,0:T(8,128)(2,1)S(1)}, bf16[1088,256]{1,0:T(8,128)(2,1)S(1)}, u32[]{:S(2)}, u32[]{:S(2)}) collective-permute-start(bf16[1088,256]{1,0:T(8,128)(2,1)S(1)} %collective-permute-done.3), channel_id=1, source_target_pairs={{0,28},{4,0},{8,4},{12,8},{16,12},{20,16},{24,20},{28,24},{1,29},{... | collective-permute-start | bytes 1671176 | tf_op jit(solution)/shard_map/ppermute | solution.py:83
  147.9 31.9 %collective-permute-start.6 = (bf16[1088,256]{1,0:T(8,128)(2,1)S(1)}, bf16[1088,256]{1,0:T(8,128)(2,1)S(1)}, u32[]{:S(2)}, u32[]{:S(2)}) collective-permute-start(bf16[1088,256]{1,0:T(8,128)(2,1)S(1)} %collective-permute-done.4), channel_id=1, source_target_pairs={{0,4},{4,8},{8,12},{12,16},{16,20},{20,24},{24,28},{28,0},{1,5},{5... | collective-permute-start | bytes 1671176 | tf_op jit(solution)/shard_map/ppermute | solution.py:78
  219.9 55.2 %all-to-all-start = ((bf16[4,2048,256]{2,1,0:T(8,128)(2,1)}), bf16[4,2048,256]{2,1,0:T(8,128)(2,1)}, u32[]{:S(2)}, u32[]{:S(2)}) async-start(bf16[4,2048,256]{2,1,0:T(8,128)(2,1)} %broadcast_select_fusion), calls=%async_computation.1 | async-start | bytes 8388608 | tf_op jit(solution)/shard_map/all_to_all | solution.py:89
Sparse Core Ops, SparseCore 0:
  42.5 213.0 reduce-scatter.1
